TPU v7x, 256 devices: a whole 4x4x8 slice. The times are simulated.
256 devices in a mesh: row: 32 (over y, z), col: 8 (over x, core).
Axes of the slice: x: 4, y: 4, z: 8, core: 2. Of those that a mesh axis runs over, the one named last changes fastest.
Arguments:
- grams: bfloat16 [4, 3584, 3584], P(None, 'row', 'col'), as said below
- weights: bfloat16 [4, 3584, 7168], P(None, 'row', 'col'), may hold values from -6 to 6
Outputs:
- merged: float32 [3584, 7168], P('row', 'col')
- residual: float32 [3584, 7168], P('row', 'col')
Inputs may be any that keep to these rules, and one draw needn't show every extreme that they name: `grams`: each of the 4 matrices is symmetric and positive definite.
All inputs are finite; a program needn't handle non-finite values.
Results may differ from a plain program's by a relative error of at most 0.012.
The roundings to bfloat16 on the way count: a program that leaves them out, or rounds other values in their place, can miss the bound.
Values may be sent and summed in bfloat16 or wider, within the bound.
A program may use at most 256 MiB of HBM per device.

v0:
```python
import jax
import jax.numpy as jnp
from jax import lax
from jax.sharding import Mesh
from jax.sharding import PartitionSpec as P

ITERS = 2
ROW = ("row_0", "row_1")


def sum_by_axis(so_far, axes):
    for axis in axes:
        so_far = lax.psum_scatter(so_far, axis, scatter_dimension=0, tiled=True)
    return so_far


def sent_to_all(x, axis):
    copies = jnp.broadcast_to(x, (lax.axis_size(axis), *x.shape))
    return lax.all_to_all(copies, axis, split_axis=0, concat_axis=0, tiled=True)


def of_everyone(x, axis):
    return sent_to_all(x, axis).sum(axis=0)


def together(arrays, axis):
    ravelled, at, done = (jnp.concatenate([a.reshape(-1) for a in arrays]), 0, [])
    so_far = of_everyone(ravelled, axis)
    for a in arrays:
        done.append(so_far[at : at + a.size].reshape(a.shape))
        at += a.size
    return tuple(done)


def shards(grams, weights):
    slab_rows = grams.shape[1]
    col_count = weights.shape[2]
    first_row = lax.axis_index(ROW) * slab_rows
    high = lax.Precision.HIGHEST
    gram_slabs = lax.all_gather(grams, "col", axis=2, tiled=True)
    gram_total = jnp.sum(gram_slabs, axis=0, dtype=jnp.float32)
    square_block = lax.dynamic_slice_in_dim(gram_slabs, first_row, slab_rows, gram_slabs.ndim - 1)
    diag_total = jnp.einsum(
        "mr,mrc->rc",
        jnp.diagonal(square_block, axis1=-2, axis2=-1).astype(jnp.float32),
        weights.astype(jnp.float32),
    )
    product = sum_by_axis(
        jnp.einsum("mrk,mrc->kc", gram_slabs, weights, preferred_element_type=jnp.float32), ROW
    )
    right_side = 0.9 * product + 0.1 * diag_total
    total_diag = jnp.diagonal(lax.dynamic_slice_in_dim(gram_total, first_row, slab_rows, 1))
    merged = jnp.zeros((slab_rows, col_count), jnp.float32)
    residual = right_side
    direction = right_side
    for iteration in range(ITERS):
        rounded = direction.astype(jnp.bfloat16)
        shard_piece = lax.all_gather(rounded, ROW, axis=0, tiled=True)
        add_columns = lax.slice_in_dim(gram_total, 0, shard_piece.shape[0], axis=1)
        mapped = jnp.zeros((slab_rows, col_count), jnp.float32) + jnp.dot(
            add_columns, shard_piece.astype(jnp.float32), precision=high
        )
        mapped = 0.9 * mapped + 0.1 * total_diag[:, None] * rounded.astype(jnp.float32)
        curvature, cross_term, square, norm_now = together(
            (
                jnp.sum(direction * mapped, axis=0),
                jnp.sum(residual * mapped, axis=0),
                jnp.sum(mapped * mapped, axis=0),
                jnp.sum(residual * residual, axis=0),
            ),
            ROW,
        )
        step_length = norm_now / curvature
        merged = merged + step_length * direction
        residual = residual - step_length * mapped
        if iteration + 1 < ITERS:
            norm_next = (
                norm_now - 2.0 * step_length * cross_term + step_length * step_length * square
            )
            direction = residual + norm_next / norm_now * direction
    return (merged, residual)


def solution(mesh):
    torus = Mesh(mesh.devices.reshape(4, 8, mesh.shape["col"]), ("row_0", "row_1", "col"))
    in_specs = (P(None, ROW, "col"), P(None, ROW, "col"))
    out_specs = (P(ROW, "col"), P(ROW, "col"))
    return jax.shard_map(
        shards, mesh=torus, in_specs=in_specs, out_specs=out_specs, check_vma=False
    )
```

profile of v0, /device:TPU:32, one launch (start us, length us, event | category | flops | bytes accessed | tf_op | source)
XLA Modules:
  0.0 467.3 jit_solution(11836406161750740182)
XLA Ops:
  7.2 0.0 copy-start
  7.2 0.0 all-gather.4.cloned.1.call-start
  7.2 2.1 copy.14
  9.3 0.0 all-gather.4.cloned.1.call-update
  9.3 0.0 reduce-scatter.3.cloned.1.call-start
  9.4 35.5 %all-gather.4.cloned.1.call-done = bf16[4,112,3584]{1,2,0:T(8,128)(2,1)} async-done(((bf16[4,112,448]{1,2,0:T(8,128)(2,1)}), bf16[4,112,3584]{1,2,0:T(8,128)(2,1)}) %all-gather.4.cloned.1.call-update) | async-done | bytes 3211280 | tf_op jit(solution)/shard_map/all_gather | solution.py:40
  44.9 0.0 copy-done
  44.9 8.9 %convolution_bitcast_fusion = f32[3584,896]{1,0:T(8,128)} fusion(bf16[4,112,3584]{1,2,0:T(8,128)(2,1)} %all-gather.4.cloned.1.call-done, bf16[4,112,896]{2,1,0:T(8,128)(2,1)S(1)} %copy-done), kind=kOutput, calls=%fused_computation.2 | convolution fusion | flops 2877292544 | bytes 16859136 | tf_op jit(solution)/shard_map/mrk,mrc->kc/dot_general | solution.py:49
  53.7 0.0 reduce-scatter.3.cloned.1.call-update
  53.8 0.0 reduce-scatter.5.cloned.1.call-start
  53.8 119.3 %reduce-scatter.3.cloned.1.call-done = f32[896,896]{1,0:T(8,128)} async-done(((f32[3584,896]{1,0:T(8,128)}), f32[896,896]{1,0:T(8,128)}) %reduce-scatter.3.cloned.1.call-update) | async-done | bytes 3211280 | tf_op jit(solution)/shard_map/reduce_scatter | solution.py:13
  173.1 0.0 reduce-scatter.5.cloned.1.call-update
  173.1 0.0 all-gather.6.cloned.1.call-start
  173.2 0.9 constant_dynamic-slice_fusion.1
  174.1 3.2 copy.15
  177.3 2.9 gather_fusion
  180.2 0.6 fusion.2
  180.8 41.3 %reduce-scatter.5.cloned.1.call-done = f32[112,896]{1,0:T(8,128)} async-done(((f32[896,896]{1,0:T(8,128)}), f32[112,896]{1,0:T(8,128)}) %reduce-scatter.5.cloned.1.call-update) | async-done | bytes 401424 | tf_op jit(solution)/shard_map/reduce_scatter | solution.py:13
  222.1 1.8 fusion.10
  223.9 0.0 copy-start.1
  223.9 0.0 all-gather.6.cloned.1.call-update
  223.9 0.0 all-gather.8.cloned.1.call-start
  223.9 3.0 convert_reduce_fusion
  227.0 0.1 copy.24
  227.1 1.7 gather_fusion.1
  228.8 85.2 %all-gather.6.cloned.1.call-done = bf16[3584,896]{1,0:T(8,128)(2,1)} async-done(((bf16[112,896]{1,0:T(8,128)(2,1)}), bf16[3584,896]{1,0:T(8,128)(2,1)}) %all-gather.6.cloned.1.call-update) | async-done | bytes 6422544 | tf_op jit(solution)/shard_map/all_gather | solution.py:58
  314.0 0.0 copy-done.1
  314.0 7.0 %multiply_reduce_fusion.6 = (f32[896]{0:T(1024)S(1)}, f32[896]{0:T(1024)S(1)}, f32[896]{0:T(1024)S(1)}, f32[112,896]{1,0:T(8,128)}) fusion(f32[112,896]{1,0:T(8,128)S(1)} %get-tuple-element.14, bf16[112,896]{1,0:T(8,128)(2,1)S(1)} %copy-done.1, f32[112]{0:T(128)S(1)} %broadcast_multiply_fusion, f32[112,3584]{0,1:T(8,128)S(1)} %convert_reduce_fusion, ...), kind=kOutput, calls=%fused_computation.22 | convolution fusion | flops 4316939776 | bytes 9042880 | tf_op jit(solution)/shard_map/dot_general | solution.py:60
  320.9 0.2 broadcast_in_dim.12
  321.2 21.5 %all_to_all.12 = f32[32,1,3584]{2,1,0:T(1,128)S(1)} all-to-all(f32[32,1,3584]{2,1,0:T(1,128)S(1)} %broadcast_in_dim.12), channel_id=1, replica_groups=mesh['row_0'=4,'row_1'=8,'col'=8] {'row_0','row_1'}, dimensions={0} | all-to-all | bytes 917504 | tf_op jit(solution)/shard_map/all_to_all | solution.py:19
  342.7 0.3 reduce_sum.98
  343.0 1.7 fusion.5
  344.8 0.0 all-gather.8.cloned.1.call-update
  344.8 84.9 %all-gather.8.cloned.1.call-done = bf16[3584,896]{1,0:T(8,128)(2,1)} async-done(((bf16[112,896]{1,0:T(8,128)(2,1)}), bf16[3584,896]{1,0:T(8,128)(2,1)}) %all-gather.8.cloned.1.call-update) | async-done | bytes 6422544 | tf_op jit(solution)/shard_map/all_gather | solution.py:58
  429.7 7.0 %multiply_reduce_fusion.3 = (f32[896]{0:T(1024)S(1)}, f32[896]{0:T(1024)S(1)}, f32[896]{0:T(1024)S(1)}, f32[896]{0:T(1024)S(1)}, f32[112,896]{1,0:T(8,128)}) fusion(f32[112,896]{1,0:T(8,128)S(1)} %get-tuple-element.10, f32[112,896]{1,0:T(8,128)S(1)} %get-tuple-element.14, f32[896]{0:T(1024)S(1)} %get-tuple-element.11, ...), kind=kOutput, calls=%fused_computation.17 | convolution fusion | flops 4317340160 | bytes 9451456 | tf_op jit(solution)/shard_map/dot_general | solution.py:60
  436.7 0.2 broadcast_in_dim.13
  437.0 21.5 %all_to_all.13 = f32[32,1,3584]{2,1,0:T(1,128)S(1)} all-to-all(f32[32,1,3584]{2,1,0:T(1,128)S(1)} %broadcast_in_dim.13), channel_id=1, replica_groups=mesh['row_0'=4,'row_1'=8,'col'=8] {'row_0','row_1'}, dimensions={0} | all-to-all | bytes 917504 | tf_op jit(solution)/shard_map/all_to_all | solution.py:19
  458.5 0.3 reduce_sum.103
  458.8 2.0 multiply_subtract_fusion
  (7 shorter events, 0.1 us)
Async XLA Ops:
  7.2 37.7 %copy-start = (bf16[4,112,896]{2,1,0:T(8,128)(2,1)S(1)}, bf16[4,112,896]{2,1,0:T(8,128)(2,1)}, u32[]{:S(2)}) copy-start(bf16[4,112,896]{2,1,0:T(8,128)(2,1)} %param.3) | copy-start | bytes 2408452
  7.2 37.7 %all-gather.4.cloned.1.call-start = ((), (), s32[]{:S(2)}) async-start(), calls=%async_computation.4 | async-start | bytes 4128768 | tf_op jit(solution)/shard_map/all_gather | solution.py:40
  9.3 163.8 %reduce-scatter.3.cloned.1.call-start = ((), (), s32[]{:S(2)}) async-start(), calls=%async_computation.5 | async-start | bytes 16056320 | tf_op jit(solution)/shard_map/reduce_scatter | solution.py:13
  53.8 168.3 %reduce-scatter.5.cloned.1.call-start = ((), (), s32[]{:S(2)}) async-start(), calls=%async_computation.6 | async-start | bytes 3612672 | tf_op jit(solution)/shard_map/reduce_scatter | solution.py:13
  173.1 140.9 %all-gather.6.cloned.1.call-start = ((), (), s32[]{:S(2)}) async-start(), calls=%async_computation.7 | async-start | bytes 6623232 | tf_op jit(solution)/shard_map/all_gather | solution.py:58
  223.9 90.1 %copy-start.1 = (bf16[112,896]{1,0:T(8,128)(2,1)S(1)}, bf16[112,896]{1,0:T(8,128)(2,1)}, u32[]{:S(2)}) copy-start(bf16[112,896]{1,0:T(8,128)(2,1)} %get-tuple-element.13) | copy-start | bytes 602116
  223.9 205.8 %all-gather.8.cloned.1.call-start = ((), (), s32[]{:S(2)}) async-start(), calls=%async_computation.8 | async-start | bytes 6623232 | tf_op jit(solution)/shard_map/all_gather | solution.py:58
Sparse Core Ops, SparseCore 0:
  9.8 34.9 all-gather.3
  53.9 119.1 reduce-scatter.2
  175.6 46.4 reduce-scatter.4
  225.1 88.8 all-gather.5
  344.9 84.7 all-gather.7
where the time goes:
time: 468 us; the launch traced here: 467 us
  waiting for transfers between devices  366 us (78%)
  blocking collectives  43.1 us (9%)
  matrix products  23.4 us (5%)
  between operations  13.9 us (3%)
  local copies, waits for them, and re-layouts  11.4 us (2%)
  other arithmetic  9.11 us (2%)
    all_gather x2, waiting for transfers between devices, shards(): shard_piece = lax.all_gather(rounded, ROW, axis=0, tiled=True)  170 us
    reduce_scatter x2, waiting for transfers between devices, sum_by_axis(): so_far = lax.psum_scatter(so_far, axis, scatter_dimension=0, tiled=True)  161 us
    all_to_all x2, blocking collectives, sent_to_all(): return lax.all_to_all(copies, axis, split_axis=0, concat_axis=0, tiled=True)  43.1 us
    all_gather x1, waiting for transfers between devices, shards(): gram_slabs = lax.all_gather(grams, 'col', axis=2, tiled=True)  35.5 us
    dot_general x2, matrix products, shards(): jnp.dot(add_columns, shard_piece.astype(jnp.float32), precision=high)  14 us
  transfers between devices with their start and end apart: 5, of which 5 were waited for; matrix products, arithmetic and copies ran while one was open for 3% of the time, Pallas kernels for 0%

commit v1 on v0

--- a/solution.py
+++ b/solution.py
@@ -37,7 +37,21 @@
     col_count = weights.shape[2]
     first_row = lax.axis_index(ROW) * slab_rows
     high = lax.Precision.HIGHEST
-    gram_slabs = lax.all_gather(grams, "col", axis=2, tiled=True)
+    ways, here, step = (lax.axis_size("col"), lax.axis_index("col"), grams.shape[2])
+    shape = [n * ways if d == 2 else n for d, n in enumerate(grams.shape)]
+    full = lax.dynamic_update_slice_in_dim(
+        jnp.zeros(shape, grams.dtype), grams, here * step, axis=2
+    )
+    going_up = going_down = grams
+    for far in range(1, ways // 2 + 1):
+        going_up = lax.ppermute(going_up, "col", [(d, (d + 1) % ways) for d in range(ways)])
+        full = lax.dynamic_update_slice_in_dim(full, going_up, (here - far) % ways * step, axis=2)
+        if 2 * far < ways:
+            going_down = lax.ppermute(going_down, "col", [(d, (d - 1) % ways) for d in range(ways)])
+            full = lax.dynamic_update_slice_in_dim(
+                full, going_down, (here + far) % ways * step, axis=2
+            )
+    gram_slabs = full
     gram_total = jnp.sum(gram_slabs, axis=0, dtype=jnp.float32)
     square_block = lax.dynamic_slice_in_dim(gram_slabs, first_row, slab_rows, gram_slabs.ndim - 1)
     diag_total = jnp.einsum(

time: 468 us -> 718 us (1.53)
  local copies, waits for them, and re-layouts: 11.4 us -> 283 us
  waiting for transfers between devices: 366 us -> 303 us
  other arithmetic: 9.11 us -> 39.7 us
  starting transfers between devices: 0.2 us -> 9.1 us
    dynamic_update_slice x0 -> x9, local copies, waits for them, and re-layouts: none -> 159 us  [the longest x5 121 us: shards(): lax.dynamic_update_slice_in_dim(full, going_up, (here - far) % ways * ste...]
    ppermute x0 -> x7, local copies, waits for them, and re-layouts: none -> 69.3 us  [the longest x4 39.6 us: shards(): lax.ppermute(going_up, 'col', [(d, (d + 1) % ways) for d in range(ways)])]
    all_gather x1 -> x0, waiting for transfers between devices: 35.5 us -> none  [shards(): gram_slabs = lax.all_gather(grams, 'col', axis=2, tiled=True)]
    broadcast_in_dim x0 -> x1, local copies, waits for them, and re-layouts: none -> 35.4 us  [shards(): jnp.zeros(shape, grams.dtype)]
    all_gather x2, waiting for transfers between devices: 170 us -> 139 us  [shards(): shard_piece = lax.all_gather(rounded, ROW, axis=0, tiled=True)]
    reduce_sum x1, other arithmetic: 3.03 us -> 33.7 us  [shards(): gram_total = jnp.sum(gram_slabs, axis=0, dtype=jnp.float32)]
    ppermute x0 -> x7, starting transfers between devices: none -> 8.76 us  [the longest x3 8.74 us: shards(): lax.ppermute(going_down, 'col', [(d, (d - 1) % ways) for d in range(ways)])]
    unnamed x6 -> x7, local copies, waits for them, and re-layouts: 2.16 us -> 10.9 us
  transfers between devices with their start and end apart: 5 -> 11, of which waited for: 5 -> 4; matrix products, arithmetic and copies ran while one was open for 3% -> 31% of each run, Pallas kernels for 0% -> 0%
where the time goes in v1:
time: 718 us; the launch traced here: 715 us
  waiting for transfers between devices  303 us (42%)
  local copies, waits for them, and re-layouts  283 us (39%)
  blocking collectives  43.1 us (6%)
  other arithmetic  39.7 us (6%)
  matrix products  22.7 us (3%)
  between operations  13.9 us (2%)
  starting transfers between devices  9.1 us (1%)
    reduce_scatter x2, waiting for transfers between devices, sum_by_axis(): so_far = lax.psum_scatter(so_far, axis, scatter_dimension=0, tiled=True)  164 us
    all_gather x2, waiting for transfers between devices, shards(): shard_piece = lax.all_gather(rounded, ROW, axis=0, tiled=True)  139 us
    dynamic_update_slice x5, local copies, waits for them, and re-layouts, shards(): lax.dynamic_update_slice_in_dim(full, going_up, (here - far) % ways * ste...  121 us
    all_to_all x2, blocking collectives, sent_to_all(): return lax.all_to_all(copies, axis, split_axis=0, concat_axis=0, tiled=True)  43.1 us
    ppermute x4, local copies, waits for them, and re-layouts, shards(): lax.ppermute(going_up, 'col', [(d, (d + 1) % ways) for d in range(ways)])  39.6 us
    broadcast_in_dim x1, local copies, waits for them, and re-layouts, shards(): jnp.zeros(shape, grams.dtype)  35.4 us
    reduce_sum x1, other arithmetic, shards(): gram_total = jnp.sum(gram_slabs, axis=0, dtype=jnp.float32)  33.7 us
    dynamic_update_slice x3, local copies, waits for them, and re-layouts, shards(): lax.dynamic_update_slice_in_dim(full, going_down, (here + far) % ways * s...  32.2 us
  transfers between devices with their start and end apart: 11, of which 4 were waited for; matrix products, arithmetic and copies ran while one was open for 31% of the time, Pallas kernels for 0%

profile of v1, /device:TPU:32, one launch (start us, length us, event | category | flops | bytes accessed | tf_op | source)
XLA Modules:
  0.0 715.0 jit_solution(9014105755771254379)
XLA Ops:
  7.2 0.0 reduce-scatter.3.cloned.1.call-start
  7.2 2.9 collective-permute-start.1
  10.2 10.8 %copy.30 = bf16[4,112,448]{0,2,1:T(8,128)(2,1)} copy(bf16[4,112,448]{2,1,0:T(8,128)(2,1)} %param.2) | data formatting | bytes 802816 | tf_op args[0]
  21.0 35.4 %broadcast_in_dim.14 = bf16[4,112,3584]{0,2,1:T(8,128)(2,1)} broadcast(bf16[]{:T(256)} %constant.70.clone.1), dimensions={} | broadcast | bytes 3211266 | tf_op jit(solution)/shard_map/broadcast_in_dim | solution.py:43
  56.4 5.4 constant_dynamic-update-slice_fusion.7
  61.8 9.9 %copy.31 = bf16[4,112,448]{0,2,1:T(8,128)(2,1)} copy(bf16[4,112,448]{2,1,0:T(8,128)(2,1)S(1)} %collective-permute-done) | data formatting | bytes 802816 | tf_op jit(solution)/shard_map/ppermute | solution.py:47
  71.7 10.7 %constant_dynamic-update-slice_fusion.6 = bf16[4,112,3584]{0,2,1:T(8,128)(2,1)} fusion(bf16[4,112,3584]{0,2,1:T(8,128)(2,1)} %constant_dynamic-update-slice_fusion.7, bf16[4,112,448]{0,2,1:T(8,128)(2,1)} %copy.31, s32[]{:T(128)S(6)} %select_n.69), kind=kLoop, calls=%fused_computation.42 | loop fusion | bytes 25690116 | tf_op jit(solution)/shard_map/dynamic_update_slice | solution.py:48
  82.4 9.9 %copy.32 = bf16[4,112,448]{0,2,1:T(8,128)(2,1)} copy(bf16[4,112,448]{2,1,0:T(8,128)(2,1)S(1)} %collective-permute-done.1) | data formatting | bytes 802816 | tf_op jit(solution)/shard_map/ppermute | solution.py:50
  92.3 10.6 %constant_dynamic-update-slice_fusion.5 = bf16[4,112,3584]{0,2,1:T(8,128)(2,1)} fusion(bf16[4,112,3584]{0,2,1:T(8,128)(2,1)} %constant_dynamic-update-slice_fusion.6, bf16[4,112,448]{0,2,1:T(8,128)(2,1)} %copy.32, s32[]{:T(128)S(6)} %select_n.71), kind=kLoop, calls=%fused_computation.41 | loop fusion | bytes 25690116 | tf_op jit(solution)/shard_map/dynamic_update_slice | solution.py:51
  103.0 3.0 collective-permute-start.3
  106.0 9.9 %copy.33 = bf16[4,112,448]{0,2,1:T(8,128)(2,1)} copy(bf16[4,112,448]{2,1,0:T(8,128)(2,1)S(1)} %collective-permute-done.2) | data formatting | bytes 802816 | tf_op jit(solution)/shard_map/ppermute | solution.py:47
  115.9 10.7 %constant_dynamic-update-slice_fusion.4 = bf16[4,112,3584]{0,2,1:T(8,128)(2,1)} fusion(bf16[4,112,3584]{0,2,1:T(8,128)(2,1)} %constant_dynamic-update-slice_fusion.5, bf16[4,112,448]{0,2,1:T(8,128)(2,1)} %copy.33, s32[]{:T(128)S(6)} %select_n.73), kind=kLoop, calls=%fused_computation.40 | loop fusion | bytes 25690116 | tf_op jit(solution)/shard_map/dynamic_update_slice | solution.py:48
  126.6 9.9 %copy.34 = bf16[4,112,448]{0,2,1:T(8,128)(2,1)} copy(bf16[4,112,448]{2,1,0:T(8,128)(2,1)S(1)} %collective-permute-done.3) | data formatting | bytes 802816 | tf_op jit(solution)/shard_map/ppermute | solution.py:50
  136.6 10.8 %constant_dynamic-update-slice_fusion.3 = bf16[4,112,3584]{0,2,1:T(8,128)(2,1)} fusion(bf16[4,112,3584]{0,2,1:T(8,128)(2,1)} %constant_dynamic-update-slice_fusion.4, bf16[4,112,448]{0,2,1:T(8,128)(2,1)} %copy.34, s32[]{:T(128)S(6)} %select_n.75), kind=kLoop, calls=%fused_computation.39 | loop fusion | bytes 25690116 | tf_op jit(solution)/shard_map/dynamic_update_slice | solution.py:51
  147.3 2.8 collective-permute-start.5
  150.1 9.9 %copy.35 = bf16[4,112,448]{0,2,1:T(8,128)(2,1)} copy(bf16[4,112,448]{2,1,0:T(8,128)(2,1)S(1)} %collective-permute-done.4) | data formatting | bytes 802816 | tf_op jit(solution)/shard_map/ppermute | solution.py:47
  160.0 10.7 %constant_dynamic-update-slice_fusion.2 = bf16[4,112,3584]{0,2,1:T(8,128)(2,1)} fusion(bf16[4,112,3584]{0,2,1:T(8,128)(2,1)} %constant_dynamic-update-slice_fusion.3, bf16[4,112,448]{0,2,1:T(8,128)(2,1)} %copy.35, s32[]{:T(128)S(6)} %select_n.77), kind=kLoop, calls=%fused_computation.38 | loop fusion | bytes 25690116 | tf_op jit(solution)/shard_map/dynamic_update_slice | solution.py:48
  170.8 9.9 %copy.36 = bf16[4,112,448]{0,2,1:T(8,128)(2,1)} copy(bf16[4,112,448]{2,1,0:T(8,128)(2,1)S(1)} %collective-permute-done.5) | data formatting | bytes 802816 | tf_op jit(solution)/shard_map/ppermute | solution.py:50
  180.7 10.8 %constant_dynamic-update-slice_fusion.1 = bf16[4,112,3584]{0,2,1:T(8,128)(2,1)} fusion(bf16[4,112,3584]{0,2,1:T(8,128)(2,1)} %constant_dynamic-update-slice_fusion.2, bf16[4,112,448]{0,2,1:T(8,128)(2,1)} %copy.36, s32[]{:T(128)S(6)} %select_n.79), kind=kLoop, calls=%fused_computation.37 | loop fusion | bytes 25690116 | tf_op jit(solution)/shard_map/dynamic_update_slice | solution.py:51
  191.5 9.9 %copy.37 = bf16[4,112,448]{0,2,1:T(8,128)(2,1)} copy(bf16[4,112,448]{2,1,0:T(8,128)(2,1)S(1)} %collective-permute-done.6) | data formatting | bytes 802816 | tf_op jit(solution)/shard_map/ppermute | solution.py:47
  201.4 10.7 %constant_dynamic-update-slice_fusion = bf16[4,112,3584]{0,2,1:T(8,128)(2,1)} fusion(bf16[4,112,3584]{0,2,1:T(8,128)(2,1)} %constant_dynamic-update-slice_fusion.1, bf16[4,112,448]{0,2,1:T(8,128)(2,1)} %copy.37, s32[]{:T(128)S(6)} %select_n.81), kind=kLoop, calls=%fused_computation.36 | loop fusion | bytes 25690116 | tf_op jit(solution)/shard_map/dynamic_update_slice | solution.py:48
  212.1 78.5 %copy.38 = bf16[4,112,3584]{2,1,0:T(8,128)(2,1)} copy(bf16[4,112,3584]{0,2,1:T(8,128)(2,1)} %constant_dynamic-update-slice_fusion) | data formatting | bytes 6422528 | tf_op jit(solution)/shard_map/dynamic_update_slice | solution.py:48
  290.6 8.8 %convolution_bitcast_fusion = f32[3584,896]{1,0:T(8,128)} fusion(bf16[4,112,3584]{2,1,0:T(8,128)(2,1)} %copy.38, bf16[4,112,896]{2,1,0:T(8,128)(2,1)S(1)} %copy-done), kind=kOutput, calls=%fused_computation.3 | convolution fusion | flops 2877292544 | bytes 16859136 | tf_op jit(solution)/shard_map/mrk,mrc->kc/dot_general | solution.py:63
  299.4 0.0 reduce-scatter.5.cloned.1.call-start
  299.5 122.0 %reduce-scatter.3.cloned.1.call-done = f32[896,896]{1,0:T(8,128)} async-done(((f32[3584,896]{1,0:T(8,128)}), f32[896,896]{1,0:T(8,128)}) %reduce-scatter.3.cloned.1.call-update) | async-done | bytes 3211280 | tf_op jit(solution)/shard_map/reduce_scatter | solution.py:13
  421.4 0.0 reduce-scatter.5.cloned.1.call-update
  421.4 0.0 all-gather.3.cloned.1.call-start
  421.5 3.8 constant_dynamic-slice_fusion.1
  425.3 2.8 gather_fusion
  428.2 0.6 fusion.2
  428.8 41.6 %reduce-scatter.5.cloned.1.call-done = f32[112,896]{1,0:T(8,128)} async-done(((f32[896,896]{1,0:T(8,128)}), f32[112,896]{1,0:T(8,128)}) %reduce-scatter.5.cloned.1.call-update) | async-done | bytes 401424 | tf_op jit(solution)/shard_map/reduce_scatter | solution.py:13
  470.4 1.8 fusion.10
  472.2 0.2 all-gather.5.cloned.1.call-start
  472.4 33.7 %convert_reduce_fusion = f32[112,3584]{1,0:T(8,128)S(1)} fusion(bf16[4,112,3584]{0,2,1:T(8,128)(2,1)} %constant_dynamic-update-slice_fusion), kind=kLoop, calls=%fused_computation.2 | loop fusion | flops 2809856 | bytes 4816896 | tf_op jit(solution)/shard_map/reduce_sum | solution.py:55
  506.1 0.1 constant_dynamic-slice_fusion
  506.2 1.7 gather_fusion.1
  507.9 54.5 %all-gather.3.cloned.1.call-done = bf16[3584,896]{1,0:T(8,128)(2,1)} async-done(((bf16[112,896]{1,0:T(8,128)(2,1)}), bf16[3584,896]{1,0:T(8,128)(2,1)}) %all-gather.3.cloned.1.call-update) | async-done | bytes 6422544 | tf_op jit(solution)/shard_map/all_gather | solution.py:72
  562.4 6.6 multiply_reduce_fusion.6
  569.0 0.2 broadcast_in_dim.15
  569.2 21.5 %all_to_all.12 = f32[32,1,3584]{2,1,0:T(1,128)S(1)} all-to-all(f32[32,1,3584]{2,1,0:T(1,128)S(1)} %broadcast_in_dim.15), channel_id=1, replica_groups=mesh['row_0'=4,'row_1'=8,'col'=8] {'row_0','row_1'}, dimensions={0} | all-to-all | bytes 917504 | tf_op jit(solution)/shard_map/all_to_all | solution.py:19
  590.8 0.3 reduce_sum.98
  591.0 1.8 fusion.5
  592.8 84.9 %all-gather.5.cloned.1.call-done = bf16[3584,896]{1,0:T(8,128)(2,1)} async-done(((bf16[112,896]{1,0:T(8,128)(2,1)}), bf16[3584,896]{1,0:T(8,128)(2,1)}) %all-gather.5.cloned.1.call-update) | async-done | bytes 6422544 | tf_op jit(solution)/shard_map/all_gather | solution.py:72
  677.7 6.7 multiply_reduce_fusion.3
  684.4 0.2 broadcast_in_dim.16
  684.7 21.5 %all_to_all.13 = f32[32,1,3584]{2,1,0:T(1,128)S(1)} all-to-all(f32[32,1,3584]{2,1,0:T(1,128)S(1)} %broadcast_in_dim.16), channel_id=1, replica_groups=mesh['row_0'=4,'row_1'=8,'col'=8] {'row_0','row_1'}, dimensions={0} | all-to-all | bytes 917504 | tf_op jit(solution)/shard_map/all_to_all | solution.py:19
  706.2 0.3 reduce_sum.103
  706.5 2.0 multiply_subtract_fusion
  (26 shorter events, 0.2 us)
Async XLA Ops:
  7.2 283.5 %copy-start = (bf16[4,112,896]{2,1,0:T(8,128)(2,1)S(1)}, bf16[4,112,896]{2,1,0:T(8,128)(2,1)}, u32[]{:S(2)}) copy-start(bf16[4,112,896]{2,1,0:T(8,128)(2,1)} %param.3) | copy-start | bytes 2408452
  7.2 414.2 %reduce-scatter.3.cloned.1.call-start = ((), (), s32[]{:S(2)}) async-start(), calls=%async_computation.4 | async-start | bytes 16056320 | tf_op jit(solution)/shard_map/reduce_scatter | solution.py:13
  7.2 54.6 %collective-permute-start = (bf16[4,112,448]{2,1,0:T(8,128)(2,1)}, bf16[4,112,448]{2,1,0:T(8,128)(2,1)S(1)}, u32[]{:S(2)}, u32[]{:S(2)}) collective-permute-start(bf16[4,112,448]{2,1,0:T(8,128)(2,1)} %param.2), channel_id=1, source_target_pairs={{0,1},{1,2},{2,3},{3,4},{4,5},{5,6},{6,7},{7,0},{8,9},{9,10},{10,1... | collective-permute-start | bytes 1204232 | tf_op jit(solution)/shard_map/ppermute | solution.py:47
  7.2 75.2 %collective-permute-start.1 = (bf16[4,112,448]{2,1,0:T(8,128)(2,1)}, bf16[4,112,448]{2,1,0:T(8,128)(2,1)S(1)}, u32[]{:S(2)}, u32[]{:S(2)}) collective-permute-start(bf16[4,112,448]{2,1,0:T(8,128)(2,1)} %param.2), channel_id=1, source_target_pairs={{0,7},{1,0},{2,1},{3,2},{4,3},{5,4},{6,5},{7,6},{8,15},{9,8},{10,9... | collective-permute-start | bytes 1204232 | tf_op jit(solution)/shard_map/ppermute | solution.py:50
  21.0 35.4 %copy-start.1 = (bf16[4,112,448]{0,2,1:T(8,128)(2,1)S(1)}, bf16[4,112,448]{0,2,1:T(8,128)(2,1)}, u32[]{:S(2)}) copy-start(bf16[4,112,448]{0,2,1:T(8,128)(2,1)} %copy.30) | copy-start | bytes 1204228
  82.4 23.6 %collective-permute-start.2 = (bf16[4,112,448]{2,1,0:T(8,128)(2,1)S(1)}, bf16[4,112,448]{2,1,0:T(8,128)(2,1)S(1)}, u32[]{:S(2)}, u32[]{:S(2)}) collective-permute-start(bf16[4,112,448]{2,1,0:T(8,128)(2,1)S(1)} %collective-permute-done), channel_id=1, source_target_pairs={{0,1},{1,2},{2,3},{3,4},{4,5},{5,6},{6,7},{7,0},{8,9},{9,10},{10,1... | collective-permute-start | bytes 1204232 | tf_op jit(solution)/shard_map/ppermute | solution.py:47
  103.0 23.6 %collective-permute-start.3 = (bf16[4,112,448]{2,1,0:T(8,128)(2,1)S(1)}, bf16[4,112,448]{2,1,0:T(8,128)(2,1)S(1)}, u32[]{:S(2)}, u32[]{:S(2)}) collective-permute-start(bf16[4,112,448]{2,1,0:T(8,128)(2,1)S(1)} %collective-permute-done.1), channel_id=1, source_target_pairs={{0,7},{1,0},{2,1},{3,2},{4,3},{5,4},{6,5},{7,6},{8,15},{9,8},{10,9... | collective-permute-start | bytes 1204232 | tf_op jit(solution)/shard_map/ppermute | solution.py:50
  126.6 23.5 %collective-permute-start.4 = (bf16[4,112,448]{2,1,0:T(8,128)(2,1)S(1)}, bf16[4,112,448]{2,1,0:T(8,128)(2,1)S(1)}, u32[]{:S(2)}, u32[]{:S(2)}) collective-permute-start(bf16[4,112,448]{2,1,0:T(8,128)(2,1)S(1)} %collective-permute-done.2), channel_id=1, source_target_pairs={{0,1},{1,2},{2,3},{3,4},{4,5},{5,6},{6,7},{7,0},{8,9},{9,10},{10,1... | collective-permute-start | bytes 1204232 | tf_op jit(solution)/shard_map/ppermute | solution.py:47
  147.3 23.4 %collective-permute-start.5 = (bf16[4,112,448]{2,1,0:T(8,128)(2,1)S(1)}, bf16[4,112,448]{2,1,0:T(8,128)(2,1)S(1)}, u32[]{:S(2)}, u32[]{:S(2)}) collective-permute-start(bf16[4,112,448]{2,1,0:T(8,128)(2,1)S(1)} %collective-permute-done.3), channel_id=1, source_target_pairs={{0,7},{1,0},{2,1},{3,2},{4,3},{5,4},{6,5},{7,6},{8,15},{9,8},{10,9... | collective-permute-start | bytes 1204232 | tf_op jit(solution)/shard_map/ppermute | solution.py:50
  170.8 20.7 %collective-permute-start.6 = (bf16[4,112,448]{2,1,0:T(8,128)(2,1)S(1)}, bf16[4,112,448]{2,1,0:T(8,128)(2,1)S(1)}, u32[]{:S(2)}, u32[]{:S(2)}) collective-permute-start(bf16[4,112,448]{2,1,0:T(8,128)(2,1)S(1)} %collective-permute-done.4), channel_id=1, source_target_pairs={{0,1},{1,2},{2,3},{3,4},{4,5},{5,6},{6,7},{7,0},{8,9},{9,10},{10,1... | collective-permute-start | bytes 1204232 | tf_op jit(solution)/shard_map/ppermute | solution.py:47
  299.4 171.0 %reduce-scatter.5.cloned.1.call-start = ((), (), s32[]{:S(2)}) async-start(), calls=%async_computation.5 | async-start | bytes 3612672 | tf_op jit(solution)/shard_map/reduce_scatter | solution.py:13
  421.4 140.9 %all-gather.3.cloned.1.call-start = ((), (), s32[]{:S(2)}) async-start(), calls=%async_computation.6 | async-start | bytes 6623232 | tf_op jit(solution)/shard_map/all_gather | solution.py:72
  472.2 90.2 %copy-start.2 = (bf16[112,896]{1,0:T(8,128)(2,1)S(1)}, bf16[112,896]{1,0:T(8,128)(2,1)}, u32[]{:S(2)}) copy-start(bf16[112,896]{1,0:T(8,128)(2,1)} %get-tuple-element.13) | copy-start | bytes 602116
  472.2 205.6 %all-gather.5.cloned.1.call-start = ((), (), s32[]{:S(2)}) async-start(), calls=%async_computation.7 | async-start | bytes 6623232 | tf_op jit(solution)/shard_map/all_gather | solution.py:72
Sparse Core Ops, SparseCore 0:
  299.5 121.8 reduce-scatter.2
  424.0 46.3 reduce-scatter.4
  473.6 88.7 all-gather.2
  593.0 84.7 all-gather.4
